TPU v7x, 32 devices: a whole 2x2x4 slice. The times are simulated.
32 devices in a mesh: row: 8 (over z, x), col: 4 (over y, core).
Axes of the slice: x: 2, y: 2, z: 4, core: 2. Of those that a mesh axis runs over, the one named last changes fastest.
Arguments:
- matrix: float32 [16384, 16384], P('row', 'col'), may hold values from -300 to 300, as said below
Outputs:
- trailing: float32 [16384, 16384], P('row', 'col')
- reflectors: float32 [16384, 8], P('row')
Inputs may be any that keep to these rules, and one draw needn't show every extreme that they name: matrix is exactly symmetric.
All inputs are finite; a program needn't handle non-finite values.
Results may differ from a plain program's by a relative error of at most 0.00021.
Values sent between devices are 32-bit elements; how exact they have to be, the bound alone decides.
A program may use at most 128 MiB of HBM per device.

v0:
```python
import functools

import jax
import jax.numpy as jnp
from jax import lax
from jax.experimental import pallas as pl
from jax.experimental.pallas import tpu as pltpu
from jax.sharding import PartitionSpec as P

COLS = 8
LANES = 128
MESH = pl.DeviceIdType.MESH

def from_root(block, axis, source):
    block = jnp.where(lax.axis_index(axis) == source, block, jnp.zeros_like(block))
    return lax.psum(block, axis)


def precise_dot(operand, factor):
    return jnp.dot(
        operand, factor, precision=lax.Precision.HIGHEST, preferred_element_type=jnp.float32
    )


def local_general(matrix):
    rows_local = matrix.shape[0]
    cols_local = matrix.shape[1]
    row_index = lax.axis_index("row")
    col_index = lax.axis_index("col")
    panel = from_root(matrix[:, :COLS], "col", 0)
    whole_panel = lax.all_gather(panel, "row", axis=0, tiled=True)
    all_ids = jnp.arange(whole_panel.shape[0], dtype=jnp.int32)
    reflect = jnp.zeros((all_ids.shape[0], COLS), jnp.float32)
    companion = jnp.zeros((all_ids.shape[0], COLS), jnp.float32)
    for column in range(COLS):
        reflect_rows = lax.dynamic_slice_in_dim(reflect, row_index * rows_local, rows_local, 0)
        companion_rows = lax.dynamic_slice_in_dim(companion, row_index * rows_local, rows_local, 0)
        current = (
            whole_panel[:, column]
            - precise_dot(reflect, companion[column])
            - precise_dot(companion, reflect[column])
        )
        below_whole = jnp.where(all_ids > column, current, 0.0)
        squared = jnp.sum(below_whole * below_whole)
        leading = jnp.sum(jnp.where(all_ids == column + 1, current, 0.0))
        length = jnp.sqrt(squared)
        vector = below_whole + jnp.where(all_ids == column + 1, length, 0.0)
        scaling = 1.0 / (length * (length + leading))
        vector_rows = lax.dynamic_slice_in_dim(vector, row_index * rows_local, rows_local, 0)
        vector_cols = lax.dynamic_slice_in_dim(vector, col_index * cols_local, cols_local, 0)
        weight_comp = precise_dot(companion.T, vector)
        weight_refl = precise_dot(reflect.T, vector)
        row_image = lax.psum(precise_dot(matrix, vector_cols), "col")
        pushed = scaling * (
            row_image
            - precise_dot(reflect_rows, weight_comp)
            - precise_dot(companion_rows, weight_refl)
        )
        inner_product = lax.psum(jnp.sum(pushed * vector_rows), "row")
        update_rows = pushed - 0.5 * scaling * inner_product * vector_rows
        update = lax.all_gather(update_rows, "row", axis=0, tiled=True)
        reflect = reflect.at[:, column].set(vector)
        companion = companion.at[:, column].set(update)
    reflect_rows = lax.dynamic_slice_in_dim(reflect, row_index * rows_local, rows_local, 0)
    companion_rows = lax.dynamic_slice_in_dim(companion, row_index * rows_local, rows_local, 0)
    reflect_cols = lax.dynamic_slice_in_dim(reflect, col_index * cols_local, cols_local, 0)
    companion_cols = lax.dynamic_slice_in_dim(companion, col_index * cols_local, cols_local, 0)
    trailing = (
        matrix
        - precise_dot(reflect_rows, companion_cols.T)
        - precise_dot(companion_rows, reflect_cols.T)
    )
    return (trailing, reflect_rows)


def total(values):
    folded = jnp.sum(values, axis=0)
    return jnp.sum(jnp.sum(folded, axis=0, keepdims=True), axis=1, keepdims=True)


def pick(values, chosen):
    kept = jnp.where(chosen, values, 0.0)
    return jnp.sum(jnp.sum(kept, axis=0, keepdims=True), axis=1, keepdims=True)


def panel_kernel(
    nr, nc, a_hbm, left_ref, right_ref, a,
    raw, mine, panel, acc, part, arrived, image, vecs, comps, nxt, corr,
    load_sem, scatter_sem, raw_sem, psend_sem, precv_sem,
    send1_sem, recv1_sem, send2_sem, recv2_sem,
):
    r = lax.axis_index("row")
    c = lax.axis_index("col")
    n = nr * nc
    rows, cols = a.shape
    quarter = rows // nc
    width = cols // nr
    subs = quarter // LANES
    tiles = cols // LANES
    here = r * nc + c

    def flip(t):
        return t + 1 - 2 * lax.rem(t, 2)

    def turn(i):
        t = lax.rem(c + 2 * (nc // 2 - 1 - i // 2), nc)
        own = i >= nc - 2
        second = lax.rem(i, 2) == 1
        first_of = jnp.where(own, flip(c), t)
        second_of = jnp.where(own, c, flip(t))
        return jnp.where(second, second_of, first_of)

    def load(i):
        at = pl.ds(pl.multiple_of(turn(i) * quarter, quarter), quarter)
        return pltpu.make_async_copy(a_hbm.at[at], a.at[at], load_sem.at[i])

    def rowcopy(q):
        at = pl.ds(pl.multiple_of(q * width, width), width)
        return a_hbm.at[pl.ds(0, COLS), at]

    @pl.when(r == 0)
    def _():
        pltpu.make_async_copy(rowcopy(0), raw, raw_sem).start()

    for i in range(nc):
        load(i).start()

    barrier = pltpu.get_barrier_semaphore()

    def greet(d, carry):
        t = lax.rem(here + d, n)
        pl.semaphore_signal(barrier, inc=1, device_id=(t // nc, lax.rem(t, nc)), device_id_type=MESH)
        return carry

    lax.fori_loop(1, n, greet, 0)

    def clear(k, carry):
        vecs[k] = jnp.zeros(vecs.shape[1:], jnp.float32)
        comps[k] = jnp.zeros(comps.shape[1:], jnp.float32)
        return carry

    lax.fori_loop(0, COLS + 1, clear, 0)
    pl.semaphore_wait(barrier, n - 1)

    def scatter(q):
        return pltpu.make_async_remote_copy(
            src_ref=rowcopy(q), dst_ref=raw, send_sem=scatter_sem.at[q], recv_sem=raw_sem,
            device_id=(q, c), device_id_type=MESH,
        )

    @pl.when(r == 0)
    def _():
        for q in range(1, nr):
            scatter(q).start()

    pltpu.make_async_copy(raw, raw, raw_sem).wait()
    for k in range(COLS):
        for m in range(subs):
            mine[k, m : m + 1, :] = raw[k : k + 1, m * LANES : (m + 1) * LANES]
    spot = c * nr + r
    panel[spot] = mine[...]

    def spread(d, carry):
        t = lax.rem(here + d, n)
        pltpu.make_async_remote_copy(
            src_ref=mine, dst_ref=panel.at[spot], send_sem=psend_sem, recv_sem=precv_sem,
            device_id=(t // nc, lax.rem(t, nc)), device_id_type=MESH,
        ).start()
        return carry

    lax.fori_loop(1, n, spread, 0)
    most = panel.at[pl.ds(0, n - 1)]
    pltpu.make_async_copy(most, most, precv_sem).wait()
    pltpu.make_async_copy(most, most, psend_sem).wait()

    @pl.when(r == 0)
    def _():
        for q in range(1, nr):
            scatter(q).wait_send()

    ids = lax.broadcasted_iota(jnp.int32, (subs, LANES), 0) * LANES + lax.broadcasted_iota(
        jnp.int32, (subs, LANES), 1
    )

    def reflect(column, current):
        vecs[column] = current
        head = jnp.where(ids > column, current[0], 0.0)
        vecs[column, 0] = head
        below = vecs[column]
        squared = total(below * below)
        leading = pick(head, ids == column + 1)
        length = jnp.sqrt(squared)
        vecs[column, 0] = head + jnp.where(ids == column + 1, length, 0.0)
        return 1.0 / (length * (length + leading))

    def step(j, scaling):
        vrows = [
            jnp.broadcast_to(vecs[j, c * nr + t // subs, t % subs : t % subs + 1, :], (8, LANES))
            for t in range(tiles)
        ]

        def block(i, carry):
            k = turn(i)

            @pl.when(j == 0)
            def _():
                load(i).wait()

            def group(g, inner):
                at = pl.ds(pl.multiple_of(k * quarter + g * 8, 8), 8)
                sums = [None] * 4
                for t in range(tiles):
                    term = a[at, t * LANES : (t + 1) * LANES] * vrows[t]
                    sums[t % 4] = term if sums[t % 4] is None else sums[t % 4] + term
                acc[pl.ds(pl.multiple_of(g * 8, 8), 8), :] = (sums[0] + sums[1]) + (sums[2] + sums[3])
                return inner

            lax.fori_loop(0, quarter // 8, group, 0, unroll=16)
            for m in range(subs):
                turned = acc[m * LANES : (m + 1) * LANES, :].T
                part[k, m : m + 1, :] = jnp.sum(turned, axis=0, keepdims=True)

            @pl.when(i < nc - 1)
            def _():
                first(k).start()

            return carry

        def first(k):
            return pltpu.make_async_remote_copy(
                src_ref=part.at[k], dst_ref=arrived.at[c], send_sem=send1_sem.at[k],
                recv_sem=recv1_sem.at[c], device_id=(r, k), device_id_type=MESH,
            )

        lax.fori_loop(0, nc, block, 0)
        value = part[c]

        def collect(d, value):
            k = lax.rem(c + d, nc)
            pltpu.make_async_copy(arrived.at[k], arrived.at[k], recv1_sem.at[k]).wait()
            return value + arrived[k]

        value = lax.fori_loop(1, nc, collect, value, unroll=True)
        image[j, here] = value

        def second(d, carry):
            t = lax.rem(here + d, n)
            pltpu.make_async_remote_copy(
                src_ref=image.at[j, here], dst_ref=image.at[j, here], send_sem=send2_sem,
                recv_sem=recv2_sem.at[j], device_id=(t // nc, lax.rem(t, nc)), device_id_type=MESH,
            ).start()
            return carry

        for d in sorted(range(1, n), key=lambda d: abs(d - n // 2)):
            second(d, 0)

        vector = vecs[j]
        corr[...] = jnp.zeros(corr.shape, jnp.float32)
        follow = jnp.minimum(j + 1, COLS - 1)
        nxt[...] = panel[:, follow]
        target = ids == j + 1

        def history(k, carry):
            v_k = vecs[k]
            w_k = comps[k]
            corr[...] = corr[...] + v_k * total(w_k * vecs[j]) + w_k * total(v_k * vecs[j])
            nxt[...] = nxt[...] - v_k * pick(w_k[0], target) - w_k * pick(v_k[0], target)
            return carry

        lax.fori_loop(0, j, history, 0)

        def sent(d, carry):
            k = lax.rem(c + d, nc)
            pltpu.make_async_copy(part.at[k], part.at[k], send1_sem.at[k]).wait()
            return carry

        lax.fori_loop(1, nc, sent, 0)
        rest = image.at[j, pl.ds(0, n - 1)]
        pltpu.make_async_copy(rest, rest, send2_sem).wait()
        pltpu.make_async_copy(rest, rest, recv2_sem.at[j]).wait()

        pushed = scaling * (image[j] - corr[...])
        inner_product = total(pushed * vector)
        update = pushed - (0.5 * scaling * inner_product) * vector
        comps[j] = update
        current = nxt[...] - vector * pick(update[0], target) - update * pick(vector[0], target)
        return reflect(j + 1, current)

    lax.fori_loop(0, COLS, step, reflect(0, panel[:, 0]))

    def place(dest, base, count):
        def move(p, carry):
            for m in range(subs):
                at = pl.ds(pl.multiple_of((p * subs + m) * LANES, LANES), LANES)
                for k in range(COLS):
                    dest[k : k + 1, at] = vecs[k, base + p, m : m + 1, :]
                    dest[COLS + k : COLS + k + 1, at] = comps[k, base + p, m : m + 1, :]
            return carry

        lax.fori_loop(0, count, move, 0)

    place(left_ref, r * nc, nc)
    place(right_ref, c * nr, nr)


def panel_call(nr, nc, matrix):
    rows, cols = matrix.shape
    n = nr * nc
    subs = rows // nc // LANES
    vector = (n, subs, LANES)
    f32 = jnp.float32
    vmem = pl.BlockSpec(memory_space=pltpu.VMEM)
    dma = pltpu.SemaphoreType.DMA
    return pl.pallas_call(
        functools.partial(panel_kernel, nr, nc),
        out_shape=(
            jax.ShapeDtypeStruct((2 * COLS, rows), f32),
            jax.ShapeDtypeStruct((2 * COLS, cols), f32),
            pltpu.VMEM((rows, cols), f32),
        ),
        in_specs=[pl.BlockSpec(memory_space=pl.ANY)],
        out_specs=(vmem, vmem, vmem),
        scratch_shapes=[
            pltpu.VMEM((COLS, cols // nr), f32),
            pltpu.VMEM((COLS, subs, LANES), f32),
            pltpu.VMEM((n, COLS, subs, LANES), f32),
            pltpu.VMEM((rows // nc, LANES), f32),
            pltpu.VMEM((nc, subs, LANES), f32),
            pltpu.VMEM((nc, subs, LANES), f32),
            pltpu.VMEM((COLS,) + vector, f32),
            pltpu.VMEM((COLS + 1,) + vector, f32),
            pltpu.VMEM((COLS + 1,) + vector, f32),
            pltpu.VMEM(vector, f32),
            pltpu.VMEM(vector, f32),
            dma((nc,)), dma((nr,)), dma, dma, dma,
            dma((nc,)), dma((nc,)), dma, dma((COLS,)),
        ],
        compiler_params=pltpu.CompilerParams(
            collective_id=0, has_side_effects=True, vmem_limit_bytes=8 * 1024 * 1024
        ),
    )(matrix)


def thirds(values):
    high = values.astype(jnp.bfloat16)
    rest = values - high.astype(jnp.float32)
    middle = rest.astype(jnp.bfloat16)
    low = (rest - middle.astype(jnp.float32)).astype(jnp.bfloat16)
    return high, middle, low


def trailing_kernel(left_ref, right_ref, a_ref, out_ref, refl_ref, stacked):
    @pl.when(pl.program_id(0) == 0)
    def _():
        swapped = jnp.concatenate([right_ref[COLS:, :], right_ref[:COLS, :]], axis=0)
        h, m, l = thirds(swapped)
        stacked[...] = jnp.concatenate([h, m, h, m, l, h], axis=0)

    left = left_ref[...]
    h, m, l = thirds(left)
    other = jnp.concatenate([h, h, m, m, h, l], axis=0)
    product = lax.dot_general(
        other, stacked[...], (((0,), (0,)), ((), ())), preferred_element_type=jnp.float32
    )
    at = pl.ds(pl.multiple_of(pl.program_id(0) * out_ref.shape[0], out_ref.shape[0]), out_ref.shape[0])
    out_ref[...] = a_ref[at, :] - product
    refl_ref[...] = left[:COLS, :]


def trailing_call(left, right, matrix):
    rows, cols = matrix.shape
    tile = 128
    return pl.pallas_call(
        trailing_kernel,
        grid=(rows // tile,),
        out_shape=(
            jax.ShapeDtypeStruct((rows, cols), jnp.float32),
            jax.ShapeDtypeStruct((COLS, rows), jnp.float32),
        ),
        in_specs=[
            pl.BlockSpec((2 * COLS, tile), lambda i: (0, i)),
            pl.BlockSpec((2 * COLS, cols), lambda i: (0, 0)),
            pl.BlockSpec(memory_space=pltpu.VMEM),
        ],
        out_specs=(
            pl.BlockSpec((tile, cols), lambda i: (i, 0)),
            pl.BlockSpec((COLS, tile), lambda i: (0, i)),
        ),
        scratch_shapes=[pltpu.VMEM((12 * COLS, cols), jnp.bfloat16)],
        compiler_params=pltpu.CompilerParams(
            dimension_semantics=("arbitrary",), vmem_limit_bytes=16 * 1024 * 1024
        ),
    )(left, right, matrix)


def local(nr, nc, matrix):
    rows, cols = matrix.shape
    piece = rows // nc
    if piece % LANES or piece > 8 * LANES or cols // nr != piece or nc % 2 or nr < 2:
        return local_general(matrix)
    left, right, kept = panel_call(nr, nc, matrix)
    trailing, reflectors = trailing_call(left, right, kept)
    return trailing, reflectors.T


def solution(mesh):
    return jax.shard_map(
        functools.partial(local, mesh.shape["row"], mesh.shape["col"]),
        mesh=mesh,
        in_specs=(P("row", "col"),),
        out_specs=(P("row", "col"), P("row", None)),
        check_vma=False,
    )
```

profile of v0, /device:TPU:0, one launch (start us, length us, event | category | flops | bytes accessed | tf_op | source)
XLA Modules:
  0.0 111.2 jit_solution(7803208193798097524)
XLA Ops:
  0.6 95.5 %shard_map.30 = (f32[16,2048]{1,0:T(8,128)S(1)}, f32[16,4096]{1,0:T(8,128)S(1)}, f32[2048,4096]{1,0:T(8,128)S(1)}) custom-call(f32[2048,4096]{1,0:T(8,128)} %a_hbm.1), custom_call_target="tpu_custom_call" | custom-call | tf_op jit(solution)/shard_map/pallas_call | solution.py:314
  96.2 15.1 %shard_map.31 = (f32[2048,4096]{1,0:T(8,128)}, f32[8,2048]{1,0:T(8,128)}) custom-call(f32[16,2048]{1,0:T(8,128)S(1)} %get-tuple-element.7.left_ref, f32[16,4096]{1,0:T(8,128)S(1)} %get-tuple-element.8.right_ref, f32[2048,4096]{1,0:T(8,128)S(1)} %get-tuple-element.9.a_ref), custom_call_target="tpu_custom_call" | custom-call | tf_op jit(solution)/shard_map/pallas_call | solution.py:373
where the time goes:
time: 111 us
  Pallas kernels  111 us (100%)
    pallas_call x1, Pallas kernels, panel_call(): pl.pallas_call(functools.partial(panel_kernel, nr, nc), out_shape=(jax.Sh...  95.5 us
    pallas_call x1, Pallas kernels, trailing_call(): pl.pallas_call(trailing_kernel, grid=(rows // tile,), out_shape=(jax.Shap...  15.1 us

commit v1 on v0

--- a/solution.py
+++ b/solution.py
@@ -9,6 +9,7 @@
 
 COLS = 8
 LANES = 128
+GUARD = 4.0
 MESH = pl.DeviceIdType.MESH
 
 def from_root(block, axis, source):
@@ -83,7 +84,7 @@
     return jnp.sum(jnp.sum(kept, axis=0, keepdims=True), axis=1, keepdims=True)
 
 
-def panel_kernel(
+def plain_kernel(
     nr, nc, a_hbm, left_ref, right_ref, a,
     raw, mine, panel, acc, part, arrived, image, vecs, comps, nxt, corr,
     load_sem, scatter_sem, raw_sem, psend_sem, precv_sem,
@@ -301,9 +302,10 @@
 
     place(left_ref, r * nc, nc)
     place(right_ref, c * nr, nr)
-
-
-def panel_call(nr, nc, matrix):
+    left_ref[2 * COLS :, :] = jnp.zeros((COLS, rows), jnp.float32)
+
+
+def plain_call(nr, nc, matrix):
     rows, cols = matrix.shape
     n = nr * nc
     subs = rows // nc // LANES
@@ -312,9 +314,9 @@
     vmem = pl.BlockSpec(memory_space=pltpu.VMEM)
     dma = pltpu.SemaphoreType.DMA
     return pl.pallas_call(
-        functools.partial(panel_kernel, nr, nc),
+        functools.partial(plain_kernel, nr, nc),
         out_shape=(
-            jax.ShapeDtypeStruct((2 * COLS, rows), f32),
+            jax.ShapeDtypeStruct((3 * COLS, rows), f32),
             jax.ShapeDtypeStruct((2 * COLS, cols), f32),
             pltpu.VMEM((rows, cols), f32),
         ),
@@ -336,6 +338,559 @@
             dma((nc,)), dma((nc,)), dma, dma((COLS,)),
         ],
         compiler_params=pltpu.CompilerParams(
+            collective_id=1, has_side_effects=True, vmem_limit_bytes=8 * 1024 * 1024
+        ),
+    )(matrix)
+
+
+def lane_sum(values):
+    return jnp.broadcast_to(jnp.sum(values, axis=1, keepdims=True), values.shape)
+
+
+def row_sum(values):
+    return jnp.sum(values, axis=0, keepdims=True)
+
+
+def panel_kernel(
+    nr, nc, a_hbm, left_ref, right_ref, a,
+    lanes, acc, pan_r, pan_c, pan_h, head_out,
+    v_r, w_r, y_r, m_r, p_r, q_r, z_r, base_r,
+    v_c, w_c, y_c, m_c, p_c, q_c, z_c, base_c,
+    v_h, w_h, g_old, h_old, g_new, h_new, wj_next, vj_next, keep, dots,
+    part_c, part_r, note_r, note_c,
+    load_sem, strip_sem, pan_send, pan_recv, cross_send, pan_cross, head_send, head_recv,
+    part_send, part_recv, back_send, back_recv, far_send, far_recv,
+    rows_send, rows_recv, note_send, note_r_recv, note_c_recv,
+):
+    r = lax.axis_index("row")
+    c = lax.axis_index("col")
+    n = nr * nc
+    here = r * nc + c
+    rows, cols = a.shape
+    deep = rows // LANES
+    wide = cols // LANES
+    chunks = wide // 8
+    width = cols // chunks
+    half = deep // 2
+    group = nr // (nc // 2)
+    side = lax.rem(c, 2)
+    owner = r // 2
+    f32 = jnp.float32
+
+    def load(q):
+        return pltpu.make_async_copy(
+            a_hbm.at[:, pl.ds(q * width, width)], a.at[:, pl.ds(q * width, width)], load_sem.at[q]
+        )
+
+    strip = pltpu.make_async_copy(a_hbm.at[:, pl.ds(0, LANES)], lanes, strip_sem)
+
+    @pl.when(c == 0)
+    def _():
+        strip.start()
+
+    @pl.when(c != 0)
+    def _():
+        for q in range(chunks):
+            load(q).start()
+
+    barrier = pltpu.get_barrier_semaphore()
+
+    def greet(d, carry):
+        t = lax.rem(here + d, n)
+        pl.semaphore_signal(barrier, inc=1, device_id=(t // nc, lax.rem(t, nc)), device_id_type=MESH)
+        return carry
+
+    lax.fori_loop(1, n, greet, 0)
+
+    for ref in (v_r, w_r, v_c, w_c, v_h, w_h, g_old, h_old, keep, dots, p_r, p_c):
+        ref[...] = jnp.zeros(ref.shape, f32)
+    y_r[0] = jnp.zeros(y_r.shape[1:], f32)
+    y_c[0] = jnp.zeros(y_c.shape[1:], f32)
+
+    def to(src, dst, send, recv, row, col):
+        return pltpu.make_async_remote_copy(
+            src_ref=src, dst_ref=dst, send_sem=send, recv_sem=recv,
+            device_id=(row, col), device_id_type=MESH,
+        )
+
+    def drain(ref, sem):
+        pltpu.make_async_copy(ref, ref, sem).wait()
+
+    used = pl.ds(0, COLS + 1)
+    first = pl.ds(0, 1)
+    others = pl.ds(1, COLS)
+
+    @pl.when(c == 0)
+    def _():
+        strip.wait()
+        for q in range(chunks):
+            load(q).start()
+
+        def turn(b, carry):
+            turned = lanes[pl.ds(pl.multiple_of(b * LANES, LANES), LANES), :].T
+            for k in range(COLS + 1):
+                pan_r[k, pl.ds(b, 1), :] = turned[k : k + 1, :]
+            return carry
+
+        lax.fori_loop(0, deep, turn, 0)
+
+    pl.semaphore_wait(barrier, n - 1)
+
+    @pl.when(c == 0)
+    def _():
+        for d in range(1, nc):
+            to(pan_r.at[first], pan_r.at[first], pan_send.at[d - 1], pan_recv.at[0], r, d).start()
+        for d in range(1, nc):
+            to(pan_r.at[others], pan_r.at[others], pan_send.at[nc + d - 1], pan_recv.at[1], r, d).start()
+
+    @pl.when(c != 0)
+    def _():
+        drain(pan_r.at[first], pan_recv.at[0])
+
+    def spread(source, target, width_of, send, recv):
+        for i in range(group):
+            row = (c // 2) * group + i
+            mine = jnp.logical_and(row == r, c == owner)
+
+            @pl.when(jnp.logical_not(mine))
+            def _(i=i, row=row):
+                to(source(side), target(lax.rem(r, 2), side), send.at[i], recv.at[2 * lax.rem(r, 2) + side], row, owner).start()
+
+    def collect(target, recv):
+        for kind in range(2):
+            for part in range(2):
+                mine = jnp.logical_and(r == 2 * c + kind, c == part + 2 * (r // group))
+
+                @pl.when(jnp.logical_not(mine))
+                def _(kind=kind, part=part):
+                    drain(target(kind, part), recv.at[2 * kind + part])
+
+    def spread_done(source, send):
+        for i in range(group):
+            row = (c // 2) * group + i
+            mine = jnp.logical_and(row == r, c == owner)
+
+            @pl.when(jnp.logical_not(mine))
+            def _(i=i):
+                drain(source(side), send.at[i])
+
+    def keeps_own():
+        return jnp.logical_and(c == owner, r // group == c // 2)
+
+    def piece(part):
+        return pl.ds(pl.multiple_of(part * half, half), half)
+
+    def spot(kind, part):
+        return pl.ds(pl.multiple_of(kind * deep + part * half, half), half)
+
+    def pan_source(part):
+        return pan_r.at[used, piece(part)]
+
+    def pan_target(kind, part):
+        return pan_c.at[used, spot(kind, part)]
+
+    def share_panel():
+        @pl.when(c != 0)
+        def _():
+            drain(pan_r.at[others], pan_recv.at[1])
+
+        spread(pan_source, pan_target, None, cross_send, pan_cross)
+
+        @pl.when(keeps_own())
+        def _():
+            pan_c[used, spot(lax.rem(r, 2), side)] = pan_r[used, piece(side)]
+
+        @pl.when(r == 0)
+        def _():
+            for k in range(COLS + 1):
+                head_out[k : k + 1, :] = pan_r[k, 0:1, :]
+                pan_h[k : k + 1, :] = pan_r[k, 0:1, :]
+            for d in range(1, nr):
+                to(head_out, pan_h, head_send.at[d - 1], head_recv, d, c).start()
+
+    ids_r = (
+        r * rows
+        + lax.broadcasted_iota(jnp.int32, (deep, LANES), 0) * LANES
+        + lax.broadcasted_iota(jnp.int32, (deep, LANES), 1)
+    )
+    ids_c = (
+        c * cols
+        + lax.broadcasted_iota(jnp.int32, (wide, LANES), 0) * LANES
+        + lax.broadcasted_iota(jnp.int32, (wide, LANES), 1)
+    )
+    lane1 = lax.broadcasted_iota(jnp.int32, (1, LANES), 1)
+    lane8 = lax.broadcasted_iota(jnp.int32, (8, LANES), 1)
+    row8 = lax.broadcasted_iota(jnp.int32, (8, LANES), 0)
+    lane24 = lax.broadcasted_iota(jnp.int32, (24, LANES), 1)
+    row24 = lax.broadcasted_iota(jnp.int32, (24, LANES), 0)
+
+    dom_r = (pan_r, v_r, w_r, y_r, m_r, p_r, q_r, z_r, base_r, ids_r)
+    dom_c = (pan_c, v_c, w_c, y_c, m_c, p_c, q_c, z_c, base_c, ids_c)
+
+    m_r[...] = jnp.where(ids_r > 0, pan_r[0], 0.0)
+
+    def send_notes(j, dom, note, slot, me, count, peer):
+        _, v, w, y, m, p, _, _, _, ids = dom
+        jm = jnp.maximum(j - 1, 0)
+        operand = m[...]
+        push = p[...]
+        last = v[jm]
+        for k in range(COLS):
+            dots[k : k + 1, :] = row_sum(w[k] * operand)
+            dots[COLS + k : COLS + k + 1, :] = row_sum(v[k] * operand)
+        cut = jnp.where(ids > j, last, 0.0)
+        dots[16:17, :] = row_sum(push * operand)
+        dots[17:18, :] = row_sum(push * last)
+        dots[18:19, :] = row_sum(operand * operand)
+        dots[19:20, :] = row_sum(operand * cut)
+        dots[20:21, :] = row_sum(cut * cut)
+        sums = lane_sum(dots[...])
+        note[slot, me, 0:1, :] = row_sum(jnp.where(lane24 == row24, sums, 0.0))
+        note[slot, me, 1:2, :] = y[j, 0:1, :]
+        recv = note_r_recv if count == nr else note_c_recv
+        for d in range(1, count):
+            row, col = peer(d)
+            to(note.at[slot, me], note.at[slot, me], note_send, recv.at[slot], row, col).start()
+
+    def take_notes(note, slot, count):
+        recv = note_r_recv if count == nr else note_c_recv
+        drain(note.at[slot, pl.ds(0, count - 1)], recv.at[slot])
+        drain(note.at[slot, pl.ds(0, count - 1)], note_send)
+        total = note[slot, 0, 0:1, :]
+        for k in range(1, count):
+            total = total + note[slot, k, 0:1, :]
+        spread24 = jnp.broadcast_to(total, (24, LANES))
+        return lane_sum(jnp.where(lane24 == row24, spread24, 0.0)), note[slot, 0, 1:2, :]
+
+    def settle(j, dom, out, sums, y_head):
+        jm = jnp.maximum(j - 1, 0)
+        jrow = pl.ds(jm, 1)
+        s_old = keep[0:1, :]
+        bad = keep[1:2, :]
+        pm, pv, mm, mv, vv = (sums[16 + i : 17 + i, :] for i in range(5))
+        alpha = 0.5 * s_old * pv
+        gold = g_old[...]
+        hold = h_old[...]
+        vh = v_h[...]
+        pan, v, w, y, m, p, _, _, _, ids = out
+        old = y[j]
+        s1 = jnp.zeros(old.shape, f32)
+        for k in range(COLS):
+            s1 = s1 + v[k] * gold[k : k + 1, :] + w[k] * hold[k : k + 1, :]
+        p_head = s_old * (y_head - row_sum(vh * gold + w_h[...] * hold))
+        v_head = v_h[jrow, :]
+        w_h[jrow, :] = p_head - alpha * v_head
+        wh = w_h[...]
+        now8 = lane8 == j
+        next8 = lane8 == j + 1
+        vj = lane_sum(jnp.where(now8, vh, 0.0))
+        wj = lane_sum(jnp.where(now8, wh, 0.0))
+        vn = lane_sum(jnp.where(next8, vh, 0.0))
+        wn = lane_sum(jnp.where(next8, wh, 0.0))
+        v_at = lane_sum(jnp.where(lane1 == j, v_head, 0.0))
+        p_at = lane_sum(jnp.where(lane1 == j, p_head, 0.0))
+        coef = 2.0 * alpha * v_at - p_at
+        before = row8 < j - 1
+        vjb = jnp.where(before, vj, 0.0)
+        wjb = jnp.where(before, wj, 0.0)
+        x_head = pan_h[pl.ds(j, 1), :] - row_sum(vh * wjb + wh * vjb) - p_head * v_at
+        b_head = jnp.where(lane1 > j, x_head + coef * v_head, 0.0)
+        lead = lane_sum(jnp.where(lane1 == j + 1, b_head, 0.0))
+        squared = mm + 2.0 * coef * mv + coef * coef * vv
+        length = jnp.sqrt(squared)
+        v_h[pl.ds(j, 1), :] = b_head + jnp.where(lane1 == j + 1, length, 0.0)
+        scale = 1.0 / (length * (length + lead))
+        pivot = lead + length
+        kappa = scale * pivot
+        fine = (mm + coef * coef * vv) <= GUARD * squared
+        keep[0:1, :] = scale
+        keep[1:2, :] = jnp.where(fine, bad, 1.0)
+        keep[2:3, :] = kappa
+        at_last = row8 == jm
+        v_sq = vv + v_at * v_at
+        gold = gold + jnp.where(at_last, pv - alpha * v_sq, 0.0)
+        hold = hold + jnp.where(at_last, v_sq, 0.0)
+        gn = sums[0:8, :] + jnp.where(at_last, pm - alpha * mv, 0.0) + coef * (gold - wj * v_at) + length * wn
+        hn = sums[8:16, :] + coef * (hold - vj * v_at) + length * vn
+        live = row8 < j
+        gn = jnp.where(live, gn, 0.0)
+        hn = jnp.where(live, hn, 0.0)
+        g_old[...] = gn
+        h_old[...] = hn
+
+        _, vd, wd, _, md, pd, _, _, _, ids_d = dom
+        last_d = vd[jm]
+        wd[jm] = pd[...] - alpha * last_d
+        vd[j] = (
+            md[...] + coef * jnp.where(ids_d > j, last_d, 0.0) + jnp.where(ids_d == j + 1, length, 0.0)
+        )
+
+        last = v[jm]
+        push = s_old * (old - s1)
+        w[jm] = push - alpha * last
+        s2 = jnp.zeros(old.shape, f32)
+        s3 = jnp.zeros(old.shape, f32)
+        s4 = jnp.zeros(old.shape, f32)
+        for k in range(COLS):
+            v_k = v[k]
+            w_k = w[k]
+            s2 = s2 + v_k * wjb[k : k + 1, :] + w_k * vjb[k : k + 1, :]
+            s3 = s3 + v_k * gn[k : k + 1, :] + w_k * hn[k : k + 1, :]
+            s4 = s4 + v_k * wn[k : k + 1, :] + w_k * vn[k : k + 1, :]
+        a_now = pan[j]
+        a_next = pan[j + 1]
+        x = a_now - s2 - push * v_at
+        b = jnp.where(ids > j, x + coef * last, 0.0)
+        v[j] = b + jnp.where(ids == j + 1, length, 0.0)
+        extra = coef * (old - v_at * a_now) + length * a_next
+        out[6][...] = extra
+        base = extra - s3
+        out[8][...] = base
+        out[7][...] = a_next - s4 - kappa * base
+
+    def absorb(j, out, at, value):
+        _, _, _, y, m, p, extra, z, base, ids = out
+        scale = keep[0:1, :]
+        kappa = keep[2:3, :]
+        y[j + 1, at, :] = value + extra[at, :]
+        p[at, :] = scale * (value + base[at, :])
+        return z[at, :] - kappa * value
+
+    blocks = rows // LANES
+    batch = 4
+    groups = LANES // 8
+
+    def tile(row, t):
+        return a[pl.ds(pl.multiple_of(row, 8), 8), t * LANES : (t + 1) * LANES]
+
+    def turn_rows(b):
+        for k in range(batch):
+            at = pl.ds(pl.multiple_of((b * batch + k) * LANES, LANES), LANES)
+            lanes[at, :] = jnp.broadcast_to(m_r[pl.ds(b * batch + k, 1), :], (LANES, LANES)).T
+
+    def down(q):
+        many = batch if q == 0 else 1
+
+        def block(b, sums):
+            factors = [
+                lanes[pl.ds(pl.multiple_of(b * many * LANES + g * 8, 8), 8), :]
+                for g in range(many * groups)
+            ]
+            if q == 0:
+                turn_rows(jnp.minimum(b + 1, blocks // batch - 1))
+            for g in range(many * groups):
+                row = b * many * LANES + g * 8
+                sums = tuple(
+                    sums[t] + tile(row, q * 8 + t) * factors[g] for t in range(8)
+                )
+            return sums
+
+        if q == 0:
+            turn_rows(0)
+        return lax.fori_loop(0, blocks // many, block, tuple(jnp.zeros((8, LANES), f32) for _ in range(8)))
+
+    def across(q, slot):
+        factors = [jnp.broadcast_to(m_c[q * 8 + t : q * 8 + t + 1, :], (8, LANES)) for t in range(8)]
+        final = q == chunks - 1
+        many = batch if final else 1
+
+        def fold(b):
+            for k in range(batch):
+                turned = acc[pl.ds(pl.multiple_of((b * batch + k) * LANES, LANES), LANES), :].T
+                part_r[slot, c, pl.ds(b * batch + k, 1), :] = row_sum(turned)
+
+        def block(b, carry):
+            if final:
+                fold(jnp.maximum(b - 1, 0))
+            for g in range(many * groups):
+                row = b * many * LANES + g * 8
+                at = pl.ds(pl.multiple_of(row, 8), 8)
+                terms = [tile(row, q * 8 + t) * factors[t] for t in range(8)]
+                while len(terms) > 1:
+                    terms = [terms[i] + terms[i + 1] for i in range(0, len(terms), 2)]
+                acc[at, :] = terms[0] if q == 0 else acc[at, :] + terms[0]
+            return carry
+
+        lax.fori_loop(0, blocks // many, block, 0)
+        if final:
+            fold(blocks // batch - 1)
+
+    def in_rows(d):
+        return lax.rem(r + d, nr), c
+
+    def in_cols(d):
+        return r, lax.rem(c + d, nc)
+
+    def back_source(j):
+        return y_c.at[j + 1, pl.ds(pl.multiple_of(lax.rem(r, 2) * deep, deep), deep)]
+
+    def pair(i, carry):
+        j = 2 * i
+        send_notes(j, dom_r, note_r, i, r, nr, in_rows)
+        for q in range(chunks):
+            @pl.when(i == 0)
+            def _(q=q):
+                load(q).wait()
+                if q == 1:
+                    share_panel()
+
+            sums = down(q)
+            for t in range(8):
+                part_c[i, q, r, t : t + 1, :] = row_sum(sums[t])
+            for d in range(1, nr):
+                row, col = in_rows(d)
+                mine = part_c.at[i, q, r]
+                to(mine, mine, part_send, part_recv.at[i, q], row, col).start()
+
+        @pl.when(i == 0)
+        def _():
+            collect(pan_target, pan_cross)
+
+            @pl.when(r != 0)
+            def _():
+                drain(pan_h, head_recv)
+
+        @pl.when(i > 0)
+        def _():
+            collect(lambda kind, part: y_c.at[j, spot(kind, part)], far_recv.at[i])
+            spread_done(lambda part: y_r.at[j, piece(part)], far_send)
+            drain(part_r.at[i, pl.ds(0, nc - 1)], rows_send)
+
+        sums, y_head = take_notes(note_r, i, nr)
+        settle(j, dom_r, dom_c, sums, y_head)
+
+        for q in range(chunks):
+            drain(part_c.at[i, q, pl.ds(0, nr - 1)], part_recv.at[i, q])
+            value = part_c[i, q, 0]
+            for k in range(1, nr):
+                value = value + part_c[i, q, k]
+            at = pl.ds(q * 8, 8)
+            m_c[at, :] = jnp.where(ids_c[q * 8 : q * 8 + 8, :] > j + 1, absorb(j, dom_c, at, value), 0.0)
+            if q == chunks - 1:
+                @pl.when(c == owner)
+                def _():
+                    for d in range(1, nc):
+                        to(back_source(j), y_r.at[j + 1], back_send.at[d - 1], back_recv.at[i], r, lax.rem(c + d, nc)).start()
+                    y_r[j + 1] = y_c[j + 1, pl.ds(pl.multiple_of(lax.rem(r, 2) * deep, deep), deep)]
+
+                send_notes(j + 1, dom_c, note_c, i, c, nc, in_cols)
+            across(q, i)
+
+        mine = part_r.at[i, c]
+        for d in range(1, nc):
+            row, col = in_cols(d)
+            to(mine, mine, rows_send, rows_recv.at[i], row, col).start()
+        drain(part_c.at[i, :, pl.ds(0, nr - 1)], part_send)
+
+        @pl.when(c != owner)
+        def _():
+            drain(y_r.at[j + 1], back_recv.at[i])
+
+        @pl.when(c == owner)
+        def _():
+            for d in range(1, nc):
+                drain(back_source(j), back_send.at[d - 1])
+
+        sums, y_head = take_notes(note_c, i, nc)
+        settle(j + 1, dom_c, dom_r, sums, y_head)
+        drain(part_r.at[i, pl.ds(0, nc - 1)], rows_recv.at[i])
+        value = part_r[i, 0]
+        for k in range(1, nc):
+            value = value + part_r[i, k]
+        m_r[...] = jnp.where(ids_r > j + 2, absorb(j + 1, dom_r, slice(None), value), 0.0)
+
+        def far_source(part):
+            return y_r.at[j + 2, piece(part)]
+
+        spread(far_source, lambda kind, part: y_c.at[j + 2, spot(kind, part)], None, far_send, far_recv.at[i + 1])
+
+        @pl.when(keeps_own())
+        def _():
+            y_c[j + 2, spot(lax.rem(r, 2), side)] = y_r[j + 2, piece(side)]
+
+        return carry
+
+    lax.fori_loop(0, COLS // 2, pair, 0)
+
+    last = COLS // 2
+    send_notes(COLS, dom_r, note_r, last, r, nr, in_rows)
+
+    @pl.when(c == 0)
+    def _():
+        for d in range(1, nc):
+            drain(pan_r.at[first], pan_send.at[d - 1])
+            drain(pan_r.at[others], pan_send.at[nc + d - 1])
+
+    spread_done(pan_source, cross_send)
+
+    @pl.when(r == 0)
+    def _():
+        for d in range(1, nr):
+            drain(head_out, head_send.at[d - 1])
+
+    def place(dest, values, base, blocks_of):
+        for b in range(blocks_of):
+            for k in range(COLS):
+                dest[base + k : base + k + 1, b * LANES : (b + 1) * LANES] = values[k, b : b + 1, :]
+
+    place(left_ref, v_r, 0, deep)
+    place(right_ref, v_c, 0, wide)
+    collect(lambda kind, part: y_c.at[COLS, spot(kind, part)], far_recv.at[last])
+    spread_done(lambda part: y_r.at[COLS, piece(part)], far_send)
+    drain(part_r.at[0, pl.ds(0, nc - 1)], rows_send)
+    sums, _ = take_notes(note_r, last, nr)
+    scale = keep[0:1, :]
+    alpha = 0.5 * scale * sums[17:18, :]
+    w_r[COLS - 1] = p_r[...] - alpha * v_r[COLS - 1]
+    s1 = jnp.zeros((wide, LANES), f32)
+    for k in range(COLS - 1):
+        s1 = s1 + v_c[k] * g_old[k : k + 1, :] + w_c[k] * h_old[k : k + 1, :]
+    w_c[COLS - 1] = scale * (y_c[COLS] - s1) - alpha * v_c[COLS - 1]
+    place(left_ref, w_r, COLS, deep)
+    place(right_ref, w_c, COLS, wide)
+    left_ref[2 * COLS :, :] = jnp.broadcast_to(keep[1:2, 0:1], (COLS, rows))
+
+
+def panel_call(nr, nc, matrix):
+    rows, cols = matrix.shape
+    deep, wide = rows // LANES, cols // LANES
+    chunks = wide // 8
+    f32 = jnp.float32
+    vmem = pl.BlockSpec(memory_space=pltpu.VMEM)
+    dma = pltpu.SemaphoreType.DMA
+    steps = COLS // 2
+
+    def mem(*shape):
+        return pltpu.VMEM(shape, f32)
+
+    def domain(size):
+        return [
+            mem(COLS + 1, size, LANES), mem(COLS + 1, size, LANES), mem(COLS + 1, size, LANES),
+            *(mem(size, LANES) for _ in range(5)),
+        ]
+
+    return pl.pallas_call(
+        functools.partial(panel_kernel, nr, nc),
+        out_shape=(
+            jax.ShapeDtypeStruct((3 * COLS, rows), f32),
+            jax.ShapeDtypeStruct((2 * COLS, cols), f32),
+            pltpu.VMEM((rows, cols), f32),
+        ),
+        in_specs=[pl.BlockSpec(memory_space=pl.ANY)],
+        out_specs=(vmem, vmem, vmem),
+        scratch_shapes=[
+            mem(rows, LANES), mem(rows, LANES),
+            mem(COLS + 1, deep, LANES), mem(COLS + 1, wide, LANES), mem(16, LANES), mem(16, LANES),
+            *domain(deep), *domain(wide),
+            mem(8, LANES), mem(8, LANES), mem(8, LANES), mem(8, LANES), mem(8, LANES), mem(8, LANES),
+            mem(8, LANES), mem(8, LANES), mem(8, LANES), mem(24, LANES),
+            mem(steps, chunks, nr, 8, LANES), mem(steps, nc, deep, LANES),
+            mem(steps + 1, nr, 2, LANES), mem(steps, nc, 2, LANES),
+            dma((chunks,)), dma, dma((2 * nc,)), dma((2,)), dma((nr,)), dma((4,)), dma((nr,)), dma,
+            dma, dma((steps, chunks)), dma((nc,)), dma((steps,)), dma((nr,)), dma((steps + 1, 4)),
+            dma, dma((steps,)), dma, dma((steps + 1,)), dma((steps,)),
+        ],
+        compiler_params=pltpu.CompilerParams(
             collective_id=0, has_side_effects=True, vmem_limit_bytes=8 * 1024 * 1024
         ),
     )(matrix)
@@ -349,14 +904,15 @@
     return high, middle, low
 
 
-def trailing_kernel(left_ref, right_ref, a_ref, out_ref, refl_ref, stacked):
+def trailing_kernel(left_ref, right_ref, a_ref, out_ref, refl_ref, flag_ref, stacked):
     @pl.when(pl.program_id(0) == 0)
     def _():
         swapped = jnp.concatenate([right_ref[COLS:, :], right_ref[:COLS, :]], axis=0)
         h, m, l = thirds(swapped)
         stacked[...] = jnp.concatenate([h, m, h, m, l, h], axis=0)
 
-    left = left_ref[...]
+    left = left_ref[: 2 * COLS, :]
+    flag_ref[...] = left_ref[2 * COLS :, :LANES]
     h, m, l = thirds(left)
     other = jnp.concatenate([h, h, m, m, h, l], axis=0)
     product = lax.dot_general(
@@ -376,15 +932,17 @@
         out_shape=(
             jax.ShapeDtypeStruct((rows, cols), jnp.float32),
             jax.ShapeDtypeStruct((COLS, rows), jnp.float32),
+            jax.ShapeDtypeStruct((COLS, LANES), jnp.float32),
         ),
         in_specs=[
-            pl.BlockSpec((2 * COLS, tile), lambda i: (0, i)),
+            pl.BlockSpec((3 * COLS, tile), lambda i: (0, i)),
             pl.BlockSpec((2 * COLS, cols), lambda i: (0, 0)),
             pl.BlockSpec(memory_space=pltpu.VMEM),
         ],
         out_specs=(
             pl.BlockSpec((tile, cols), lambda i: (i, 0)),
             pl.BlockSpec((COLS, tile), lambda i: (0, i)),
+            pl.BlockSpec((COLS, LANES), lambda i: (0, 0)),
         ),
         scratch_shapes=[pltpu.VMEM((12 * COLS, cols), jnp.bfloat16)],
         compiler_params=pltpu.CompilerParams(
@@ -396,10 +954,18 @@
 def local(nr, nc, matrix):
     rows, cols = matrix.shape
     piece = rows // nc
-    if piece % LANES or piece > 8 * LANES or cols // nr != piece or nc % 2 or nr < 2:
+    if rows % (16 * LANES) or cols != 2 * rows or nr != 2 * nc or nc % 2 or piece > 8 * LANES:
         return local_general(matrix)
     left, right, kept = panel_call(nr, nc, matrix)
-    trailing, reflectors = trailing_call(left, right, kept)
+    trailing, reflectors, flag = trailing_call(left, right, kept)
+
+    def again(state):
+        own, _ = lax.optimization_barrier((matrix, state[2]))
+        return trailing_call(*plain_call(nr, nc, own))
+
+    trailing, reflectors, _ = lax.while_loop(
+        lambda state: jnp.any(state[2] != 0.0), again, (trailing, reflectors, flag)
+    )
     return trailing, reflectors.T
 
 

time: 111 us -> 83.8 us (0.75)
  Pallas kernels: 111 us -> 81 us
  other arithmetic: 0 us -> 1.35 us
    pallas_call x1, Pallas kernels: 95.5 us -> 65.9 us  [panel_call(): pl.pallas_call(functools.partial(panel_kernel, nr, nc), out_shape=(jax.Sh...]
    reduce_or x0 -> x1, other arithmetic: none -> 1.35 us  [local(): jnp.any(state[2] != 0.0)]
where the time goes in v1:
time: 83.8 us; the launch traced here: 83.6 us
  Pallas kernels  81 us (97%)
  other arithmetic  1.35 us (2%)
    pallas_call x1, Pallas kernels, panel_call(): pl.pallas_call(functools.partial(panel_kernel, nr, nc), out_shape=(jax.Sh...  65.9 us
    pallas_call x1, Pallas kernels, trailing_call(): pl.pallas_call(trailing_kernel, grid=(rows // tile,), out_shape=(jax.Shap...  15.1 us

profile of v1, /device:TPU:0, one launch (start us, length us, event | category | flops | bytes accessed | tf_op | source)
XLA Modules:
  0.0 83.6 jit_solution(6250379351106580481)
XLA Ops:
  0.6 65.9 %shard_map.30 = (f32[24,2048]{1,0:T(8,128)S(1)}, f32[16,4096]{1,0:T(8,128)S(1)}, f32[2048,4096]{1,0:T(8,128)S(1)}) custom-call(f32[2048,4096]{1,0:T(8,128)} %a_hbm.1), custom_call_target="tpu_custom_call" | custom-call | tf_op jit(solution)/shard_map/pallas_call | solution.py:872
  66.5 15.1 %shard_map.31 = (f32[2048,4096]{1,0:T(8,128)}, f32[8,2048]{1,0:T(8,128)}, f32[8,128]{1,0:T(8,128)}) custom-call(f32[24,2048]{1,0:T(8,128)S(1)} %get-tuple-element.110.left_ref, f32[16,4096]{1,0:T(8,128)S(1)} %get-tuple-element.111.right_ref, f32[2048,4096]{1,0:T(8,128)S(1)} %get-tuple-element.112.a_ref), custom_call_target="tpu_custom_call" | custom-call | tf_op jit(solution)/shard_map/pallas_call | solution.py:929
  81.6 2.0 %while.15 = (f32[2048,4096]{1,0:T(8,128)}, f32[8,2048]{1,0:T(8,128)}, f32[8,128]{1,0:T(8,128)}, f32[2048,4096]{1,0:T(8,128)}) while((f32[2048,4096]{1,0:T(8,128)}, f32[8,2048]{1,0:T(8,128)}, f32[8,128]{1,0:T(8,128)}, f32[2048,4096]{1,0:T(8,128)}) %tuple.38), condition=%region_1.0_spmd, body=%region_0.0_spmd | while | flops 2047 | bytes 4129 | solution.py:966
  81.6 1.3 %compare_reduce_fusion = pred[]{:T(512)} fusion(f32[8,128]{1,0:T(8,128)} %get-tuple-element.99), kind=kLoop, calls=%fused_computation | loop fusion | flops 2047 | bytes 4097 | tf_op jit(solution)/shard_map/while/cond/reduce_or | solution.py:967

commit v2 on v1

--- a/solution.py
+++ b/solution.py
@@ -358,7 +358,7 @@
     v_c, w_c, y_c, m_c, p_c, q_c, z_c, base_c,
     v_h, w_h, g_old, h_old, g_new, h_new, wj_next, vj_next, keep, dots,
     part_c, part_r, note_r, note_c,
-    load_sem, strip_sem, pan_send, pan_recv, cross_send, pan_cross, head_send, head_recv,
+    load_sem, strip_sem, pan_send, pan_recv, cross_send, pan_cross, rest_send, pan_rest, head_send, head_recv,
     part_send, part_recv, back_send, back_recv, far_send, far_recv,
     rows_send, rows_recv, note_send, note_r_recv, note_c_recv,
 ):
@@ -417,8 +417,8 @@
         pltpu.make_async_copy(ref, ref, sem).wait()
 
     used = pl.ds(0, COLS + 1)
-    first = pl.ds(0, 1)
-    others = pl.ds(1, COLS)
+    first = pl.ds(0, 2)
+    others = pl.ds(2, COLS - 1)
 
     @pl.when(c == 0)
     def _():
@@ -483,22 +483,20 @@
     def spot(kind, part):
         return pl.ds(pl.multiple_of(kind * deep + part * half, half), half)
 
-    def pan_source(part):
-        return pan_r.at[used, piece(part)]
-
-    def pan_target(kind, part):
-        return pan_c.at[used, spot(kind, part)]
-
-    def share_panel():
+    def share_panel(part_of, send, recv):
+        spread(lambda part: pan_r.at[part_of, piece(part)], lambda kind, part: pan_c.at[part_of, spot(kind, part)], None, send, recv)
+
+        @pl.when(keeps_own())
+        def _():
+            pan_c[part_of, spot(lax.rem(r, 2), side)] = pan_r[part_of, piece(side)]
+
+    def take_panel(part_of, recv):
+        collect(lambda kind, part: pan_c.at[part_of, spot(kind, part)], recv)
+
+    def share_head():
         @pl.when(c != 0)
         def _():
             drain(pan_r.at[others], pan_recv.at[1])
-
-        spread(pan_source, pan_target, None, cross_send, pan_cross)
-
-        @pl.when(keeps_own())
-        def _():
-            pan_c[used, spot(lax.rem(r, 2), side)] = pan_r[used, piece(side)]
 
         @pl.when(r == 0)
         def _():
@@ -507,6 +505,8 @@
                 pan_h[k : k + 1, :] = pan_r[k, 0:1, :]
             for d in range(1, nr):
                 to(head_out, pan_h, head_send.at[d - 1], head_recv, d, c).start()
+
+    share_panel(first, cross_send, pan_cross)
 
     ids_r = (
         r * rows
@@ -732,19 +732,20 @@
             def _(q=q):
                 load(q).wait()
                 if q == 1:
-                    share_panel()
+                    share_head()
 
             sums = down(q)
             for t in range(8):
                 part_c[i, q, r, t : t + 1, :] = row_sum(sums[t])
-            for d in range(1, nr):
+            for d in sorted(range(1, nr), key=lambda d: abs(d - nr // 2)):
                 row, col = in_rows(d)
                 mine = part_c.at[i, q, r]
                 to(mine, mine, part_send, part_recv.at[i, q], row, col).start()
 
         @pl.when(i == 0)
         def _():
-            collect(pan_target, pan_cross)
+            share_panel(others, rest_send, pan_rest)
+            take_panel(first, pan_cross)
 
             @pl.when(r != 0)
             def _():
@@ -755,6 +756,10 @@
             collect(lambda kind, part: y_c.at[j, spot(kind, part)], far_recv.at[i])
             spread_done(lambda part: y_r.at[j, piece(part)], far_send)
             drain(part_r.at[i, pl.ds(0, nc - 1)], rows_send)
+
+        @pl.when(i == 1)
+        def _():
+            take_panel(others, pan_rest)
 
         sums, y_head = take_notes(note_r, i, nr)
         settle(j, dom_r, dom_c, sums, y_head)
@@ -821,7 +826,8 @@
             drain(pan_r.at[first], pan_send.at[d - 1])
             drain(pan_r.at[others], pan_send.at[nc + d - 1])
 
-    spread_done(pan_source, cross_send)
+    spread_done(lambda part: pan_r.at[first, piece(part)], cross_send)
+    spread_done(lambda part: pan_r.at[others, piece(part)], rest_send)
 
     @pl.when(r == 0)
     def _():
@@ -886,7 +892,7 @@
             mem(8, LANES), mem(8, LANES), mem(8, LANES), mem(24, LANES),
             mem(steps, chunks, nr, 8, LANES), mem(steps, nc, deep, LANES),
             mem(steps + 1, nr, 2, LANES), mem(steps, nc, 2, LANES),
-            dma((chunks,)), dma, dma((2 * nc,)), dma((2,)), dma((nr,)), dma((4,)), dma((nr,)), dma,
+            dma((chunks,)), dma, dma((2 * nc,)), dma((2,)), dma((nr,)), dma((4,)), dma((nr,)), dma((4,)), dma((nr,)), dma,
             dma, dma((steps, chunks)), dma((nc,)), dma((steps,)), dma((nr,)), dma((steps + 1, 4)),
             dma, dma((steps,)), dma, dma((steps + 1,)), dma((steps,)),
         ],
@@ -904,50 +910,64 @@
     return high, middle, low
 
 
-def trailing_kernel(left_ref, right_ref, a_ref, out_ref, refl_ref, flag_ref, stacked):
-    @pl.when(pl.program_id(0) == 0)
-    def _():
-        swapped = jnp.concatenate([right_ref[COLS:, :], right_ref[:COLS, :]], axis=0)
-        h, m, l = thirds(swapped)
-        stacked[...] = jnp.concatenate([h, m, h, m, l, h], axis=0)
-
-    left = left_ref[: 2 * COLS, :]
+SLOTS = 4
+
+
+def trailing_kernel(left_ref, right_ref, a_ref, out_ref, refl_ref, flag_ref, stacked, stage, sem):
+    slots, tile, _ = stage.shape
+    steps = a_ref.shape[0] // tile
+    swapped = jnp.concatenate([right_ref[COLS:, :], right_ref[:COLS, :]], axis=0)
+    h, m, l = thirds(swapped)
+    stacked[...] = jnp.concatenate([h, m, h, m, l, h], axis=0)
+
+    def copy(step, slot):
+        at = pl.ds(pl.multiple_of(step * tile, tile), tile)
+        return pltpu.make_async_copy(stage.at[slot], out_ref.at[at], sem.at[slot])
+
+    def run(step, carry):
+        slot = lax.rem(step, slots)
+
+        @pl.when(step >= slots)
+        def _():
+            copy(step - slots, slot).wait()
+
+        at = pl.ds(pl.multiple_of(step * tile, tile), tile)
+        h, m, l = thirds(left_ref[: 2 * COLS, at])
+        other = jnp.concatenate([h, h, m, m, h, l], axis=0)
+        product = lax.dot_general(
+            other, stacked[...], (((0,), (0,)), ((), ())), preferred_element_type=jnp.float32
+        )
+        stage[slot] = a_ref[at, :] - product
+        copy(step, slot).start()
+        return carry
+
+    lax.fori_loop(0, steps, run, 0)
+    refl_ref[...] = left_ref[:COLS, :]
     flag_ref[...] = left_ref[2 * COLS :, :LANES]
-    h, m, l = thirds(left)
-    other = jnp.concatenate([h, h, m, m, h, l], axis=0)
-    product = lax.dot_general(
-        other, stacked[...], (((0,), (0,)), ((), ())), preferred_element_type=jnp.float32
-    )
-    at = pl.ds(pl.multiple_of(pl.program_id(0) * out_ref.shape[0], out_ref.shape[0]), out_ref.shape[0])
-    out_ref[...] = a_ref[at, :] - product
-    refl_ref[...] = left[:COLS, :]
+    for k in range(slots):
+        step = steps - slots + k
+        copy(step, step % slots).wait()
 
 
 def trailing_call(left, right, matrix):
     rows, cols = matrix.shape
     tile = 128
+    vmem = pl.BlockSpec(memory_space=pltpu.VMEM)
     return pl.pallas_call(
         trailing_kernel,
-        grid=(rows // tile,),
         out_shape=(
             jax.ShapeDtypeStruct((rows, cols), jnp.float32),
             jax.ShapeDtypeStruct((COLS, rows), jnp.float32),
             jax.ShapeDtypeStruct((COLS, LANES), jnp.float32),
         ),
-        in_specs=[
-            pl.BlockSpec((3 * COLS, tile), lambda i: (0, i)),
-            pl.BlockSpec((2 * COLS, cols), lambda i: (0, 0)),
-            pl.BlockSpec(memory_space=pltpu.VMEM),
+        in_specs=[vmem, vmem, vmem],
+        out_specs=(pl.BlockSpec(memory_space=pl.ANY), vmem, vmem),
+        scratch_shapes=[
+            pltpu.VMEM((12 * COLS, cols), jnp.bfloat16),
+            pltpu.VMEM((min(SLOTS, rows // tile), tile, cols), jnp.float32),
+            pltpu.SemaphoreType.DMA((min(SLOTS, rows // tile),)),
         ],
-        out_specs=(
-            pl.BlockSpec((tile, cols), lambda i: (i, 0)),
-            pl.BlockSpec((COLS, tile), lambda i: (0, i)),
-            pl.BlockSpec((COLS, LANES), lambda i: (0, 0)),
-        ),
-        scratch_shapes=[pltpu.VMEM((12 * COLS, cols), jnp.bfloat16)],
-        compiler_params=pltpu.CompilerParams(
-            dimension_semantics=("arbitrary",), vmem_limit_bytes=16 * 1024 * 1024
-        ),
+        compiler_params=pltpu.CompilerParams(vmem_limit_bytes=16 * 1024 * 1024),
     )(left, right, matrix)
 
 

time: 83.8 us -> 78.6 us (0.938)
  Pallas kernels: 81 us -> 75.8 us
    pallas_call x1, Pallas kernels: 15.1 us -> 12.1 us  [trailing_call(): pl.pallas_call(trailing_kernel, out_shape=(jax.ShapeDtypeStruct((rows, co...]
    pallas_call x1, Pallas kernels: 65.9 us -> 63.7 us  [panel_call(): pl.pallas_call(functools.partial(panel_kernel, nr, nc), out_shape=(jax.Sh...]
where the time goes in v2:
time: 78.6 us; the launch traced here: 78.5 us
  Pallas kernels  75.8 us (96%)
  other arithmetic  1.35 us (2%)
    pallas_call x1, Pallas kernels, panel_call(): pl.pallas_call(functools.partial(panel_kernel, nr, nc), out_shape=(jax.Sh...  63.7 us
    pallas_call x1, Pallas kernels, trailing_call(): pl.pallas_call(trailing_kernel, out_shape=(jax.ShapeDtypeStruct((rows, co...  12.1 us

profile of v2, /device:TPU:0, one launch (start us, length us, event | category | flops | bytes accessed | tf_op | source)
XLA Modules:
  0.0 78.5 jit_solution(13693897549212101610)
XLA Ops:
  0.6 63.7 %shard_map.30 = (f32[24,2048]{1,0:T(8,128)S(1)}, f32[16,4096]{1,0:T(8,128)S(1)}, f32[2048,4096]{1,0:T(8,128)S(1)}) custom-call(f32[2048,4096]{1,0:T(8,128)} %a_hbm.1), custom_call_target="tpu_custom_call" | custom-call | tf_op jit(solution)/shard_map/pallas_call | solution.py:878
  64.4 12.1 %shard_map.31 = (f32[2048,4096]{1,0:T(8,128)}, f32[8,2048]{1,0:T(8,128)}, f32[8,128]{1,0:T(8,128)}) custom-call(f32[24,2048]{1,0:T(8,128)S(1)} %get-tuple-element.110.left_ref, f32[16,4096]{1,0:T(8,128)S(1)} %get-tuple-element.111.right_ref, f32[2048,4096]{1,0:T(8,128)S(1)} %get-tuple-element.112.a_ref), custom_call_target="tpu_custom_call" | custom-call | tf_op jit(solution)/shard_map/pallas_call | solution.py:956
  76.5 2.0 %while.15 = (f32[2048,4096]{1,0:T(8,128)}, f32[8,2048]{1,0:T(8,128)}, f32[8,128]{1,0:T(8,128)}, f32[2048,4096]{1,0:T(8,128)}) while((f32[2048,4096]{1,0:T(8,128)}, f32[8,2048]{1,0:T(8,128)}, f32[8,128]{1,0:T(8,128)}, f32[2048,4096]{1,0:T(8,128)}) %tuple.38), condition=%region_1.0_spmd, body=%region_0.0_spmd | while | flops 2047 | bytes 4129 | solution.py:986
  76.5 1.4 %compare_reduce_fusion = pred[]{:T(512)} fusion(f32[8,128]{1,0:T(8,128)} %get-tuple-element.99), kind=kLoop, calls=%fused_computation | loop fusion | flops 2047 | bytes 4097 | tf_op jit(solution)/shard_map/while/cond/reduce_or | solution.py:987
